TPU v7x, 32 devices: a whole 2x2x4 slice. The times are simulated.
32 devices in a mesh: dp: 8 (over y, x, core), mp: 4 (over z).
Axes of the slice: x: 2, y: 2, z: 4, core: 2. Of those that a mesh axis runs over, the one named last changes fastest.
Arguments:
- activations: bfloat16 [8192, 4096], P(('dp', 'mp')), may hold values from -17 to 17
- output_grads: bfloat16 [8192, 14336], P('dp', 'mp'), may hold values from -0.046875 to 0.046875
- q_start: float32 [14336, 64], P('mp'), may hold values from -6 to 6
Outputs:
- new_error: bfloat16 [32768, 14336], P('dp', 'mp')
- q_factor: float32 [14336, 64], P('mp')
All inputs are finite; a program needn't handle non-finite values.
Results may differ from a plain program's by a relative error of at most 0.01.
Values may be sent and summed in bfloat16 or wider, within the bound.
No kernel may reach another device: no remote copies, remote signals or barrier semaphores. Data moves between devices by JAX's collectives and lax.ppermute only.
A program may use at most 192 MiB of HBM per device.

v0:
```python
import jax
import jax.numpy as jnp
from jax import lax
from jax.sharding import PartitionSpec as P


def orthonormal(p_mean, gram_matrix):
    lower_tri = jnp.linalg.cholesky(gram_matrix)
    return lax.linalg.triangular_solve(
        lower_tri, p_mean, left_side=False, lower=True, transpose_a=True
    )


def split_parts(values):
    upper = values.astype(jnp.bfloat16)
    lower = (values - upper.astype(jnp.float32)).astype(jnp.bfloat16)
    return (upper, lower)


def per_device(activations, output_grads, q_start):
    highest = lax.Precision.HIGHEST
    contract_rows = (((0,), (0,)), ((), ()))
    replicas = lax.axis_size("dp")
    gathered = lax.all_gather(activations, "mp", axis=0, tiled=True)
    q_upper, q_lower = split_parts(q_start)
    projected = jnp.dot(output_grads, q_upper, preferred_element_type=jnp.float32)
    projected = projected + jnp.dot(output_grads, q_lower, preferred_element_type=jnp.float32)
    proj_upper, proj_lower = split_parts(projected)
    partial_p = lax.dot_general(
        gathered, proj_upper, contract_rows, preferred_element_type=jnp.float32
    )
    partial_p = partial_p + lax.dot_general(
        gathered, proj_lower, contract_rows, preferred_element_type=jnp.float32
    )
    gradient = lax.dot_general(
        gathered, output_grads, contract_rows, preferred_element_type=jnp.float32
    )
    p_mean = lax.psum(partial_p, ("dp", "mp")) / replicas
    gram_matrix = lax.dot_general(p_mean, p_mean, contract_rows, precision=highest)
    p_ortho = orthonormal(p_mean, gram_matrix)
    local_factor = lax.dot_general(gradient, p_ortho, contract_rows, precision=highest)
    q_factor = lax.psum(local_factor, "dp") / replicas
    decompressed = lax.dot_general(p_ortho, q_factor, (((1,), (1,)), ((), ())), precision=highest)
    new_error = (gradient - decompressed).astype(jnp.bfloat16)
    return (new_error, q_factor)


def solution(mesh):
    in_specs = (P(("dp", "mp"), None), P("dp", "mp"), P("mp", None))
    out_specs = (P("dp", "mp"), P("mp", None))
    return jax.shard_map(
        per_device, mesh=mesh, in_specs=in_specs, out_specs=out_specs, check_vma=False
    )
```

profile of v0, /device:TPU:0, one launch (start us, length us, event | category | flops | bytes accessed | tf_op | source)
XLA Modules:
  0.0 476.0 jit_solution(7713348371118286907)
XLA Ops:
  7.2 0.0 copy-start.3
  7.2 0.0 all-gather.2.cloned.1.call-start
  7.2 0.7 all-gather.2.cloned.1.call-update
  7.9 0.0 all-reduce.3.cloned.1.call-start
  8.0 0.0 copy-start.1
  8.0 5.7 %fusion.9 = f32[1024,64]{0,1:T(8,128)S(1)} fusion(bf16[1024,3584]{1,0:T(8,128)(2,1)} %param.4, f32[3584,64]{0,1:T(8,128)} %param.5), kind=kOutput, calls=%fused_computation.15 | convolution fusion | flops 469991424 | bytes 8519680 | tf_op jit(solution)/shard_map/dot_general | solution.py:26
  13.7 0.0 copy-done.3
  13.7 0.0 copy-done.1
  13.7 2.3 fusion.1
  16.0 145.9 %all-gather.2.cloned.1.call-done = bf16[1024,4096]{1,0:T(8,128)(2,1)} async-done(((bf16[256,4096]{1,0:T(8,128)(2,1)}), bf16[1024,4096]{1,0:T(8,128)(2,1)}) %all-gather.2.cloned.1.call-update) | async-done | bytes 8388624 | tf_op jit(solution)/shard_map/all_gather | solution.py:24
  161.9 0.0 copy-start
  161.9 5.1 %fusion.12 = f32[64,4096]{1,0:T(8,128)S(1)} fusion(bf16[1024,4096]{1,0:T(8,128)(2,1)} %all-gather.2.cloned.1.call-done, f32[1024,64]{0,1:T(8,128)S(1)} %fusion.1), kind=kOutput, calls=%fused_computation.18 | convolution fusion | flops 536936448 | bytes 9699328 | tf_op jit(solution)/shard_map/dot_general | solution.py:29
  167.0 0.7 copy-done
  167.7 2.5 fusion
  170.2 0.0 all-reduce.3.cloned.1.call-update
  170.3 0.2 all-reduce.5.cloned.1.call-start
  170.5 40.3 %fusion.19 = f32[4096,3584]{1,0:T(8,128)} fusion(bf16[1024,4096]{1,0:T(8,128)(2,1)} %all-gather.2.cloned.1.call-done, bf16[1024,3584]{1,0:T(8,128)(2,1)} %param.4), kind=kOutput, calls=%fused_computation.31 | convolution fusion | flops 30064771072 | bytes 74448896 | tf_op jit(solution)/shard_map/dot_general | solution.py:35
  210.8 88.4 %all-reduce.3.cloned.1.call-done = f32[4096,64]{0,1:T(8,128)} async-done(((f32[4096,64]{0,1:T(8,128)}), f32[4096,64]{0,1:T(8,128)}) %all-reduce.3.cloned.1.call-update) | async-done | bytes 1048592 | tf_op jit(solution)/shard_map/psum | solution.py:38
  299.2 2.6 fusion.4
  301.9 0.1 copy.5
  301.9 5.8 %cholesky.16 = f32[64,64]{1,0:T(8,128)S(1)} custom-call(f32[64,64]{1,0:T(8,128)S(1)} %fusion.16), custom_call_target="Cholesky" | custom-call | tf_op jit(solution)/shard_map/jit(cholesky)/cholesky | solution.py:8
  307.8 0.6 compare_reduce_fusion
  308.5 0.7 fusion.14
  309.1 4.9 %custom-call.6 = f32[1,64,64]{1,2,0:T(8,128)S(1)} custom-call(f32[1,64,64]{2,1,0:T(8,128)S(1)} %fusion.14), custom_call_target="InvertDiagBlocksLowerTriangular" | custom-call | tf_op jit(solution)/shard_map/triangular_solve | solution.py:9
  314.0 2.3 fusion.2
  316.4 43.2 %fusion.20 = f32[3584,64]{0,1:T(8,128)} fusion(f32[4096,3584]{1,0:T(8,128)} %fusion.19, f32[4096,64]{0,1:T(8,128)S(1)} %fusion.2), kind=kOutput, calls=%fused_computation.32 | convolution fusion | flops 11274289152 | bytes 60686336 | tf_op jit(solution)/shard_map/dot_general | solution.py:41
  359.5 0.0 all-reduce.5.cloned.1.call-update
  359.6 55.2 %all-reduce.5.cloned.1.call-done = f32[3584,64]{0,1:T(8,128)} async-done(((f32[3584,64]{0,1:T(8,128)}), f32[3584,64]{0,1:T(8,128)}) %all-reduce.5.cloned.1.call-update) | async-done | bytes 917520 | tf_op jit(solution)/shard_map/psum | solution.py:42
  414.8 1.2 broadcast_multiply_fusion
  416.0 0.0 copy-start.2
  416.1 53.4 %subtract_convert_fusion = bf16[4096,3584]{1,0:T(8,128)(2,1)} fusion(f32[4096,3584]{1,0:T(8,128)} %fusion.19, f32[4096,64]{0,1:T(8,128)S(1)} %fusion.2, f32[3584,64]{0,1:T(8,128)S(1)} %broadcast_multiply_fusion), kind=kOutput, calls=%fused_computation | convolution fusion | flops 11303649280 | bytes 90046464 | tf_op jit(solution)/shard_map/dot_general | solution.py:43
  469.4 0.0 copy-done.2
  (2 shorter events, 0.0 us)
Async XLA Ops:
  7.2 6.5 %copy-start.3 = (f32[3584,64]{0,1:T(8,128)S(1)}, f32[3584,64]{0,1:T(8,128)}, u32[]{:S(2)}) copy-start(f32[3584,64]{0,1:T(8,128)} %param.5) | copy-start | bytes 2752516
  7.2 154.7 %all-gather.2.cloned.1.call-start = ((), (), s32[]{:S(2)}) async-start(), calls=%async_computation | async-start | bytes 10485760 | tf_op jit(solution)/shard_map/all_gather | solution.py:24
  7.9 291.3 %all-reduce.3.cloned.1.call-start = ((), (), s32[]{:S(2)}) async-start(), calls=%async_computation.1 | async-start | bytes 2097152 | tf_op jit(solution)/shard_map/psum | solution.py:38
  8.0 5.7 %copy-start.1 = (bf16[1024,3584]{1,0:T(8,128)(2,1)S(1)}, bf16[1024,3584]{1,0:T(8,128)(2,1)}, u32[]{:S(2)}) copy-start(bf16[1024,3584]{1,0:T(8,128)(2,1)} %param.4) | copy-start | bytes 22020100
  161.9 5.8 %copy-start = (bf16[1024,4096]{1,0:T(8,128)(2,1)S(1)}, bf16[1024,4096]{1,0:T(8,128)(2,1)}, u32[]{:S(2)}) copy-start(bf16[1024,4096]{1,0:T(8,128)(2,1)} %all-gather.2.cloned.1.call-done) | copy-start | bytes 25165828
  170.3 244.5 %all-reduce.5.cloned.1.call-start = ((), (), s32[]{:S(2)}) async-start(), calls=%async_computation.2 | async-start | bytes 1835008 | tf_op jit(solution)/shard_map/psum | solution.py:42
  416.0 53.4 %copy-start.2 = (f32[3584,64]{0,1:T(8,128)}, f32[3584,64]{0,1:T(8,128)S(1)}, u32[]{:S(2)}) copy-start(f32[3584,64]{0,1:T(8,128)S(1)} %broadcast_multiply_fusion) | copy-start | bytes 2752516
Sparse Core Ops, SparseCore 0:
  9.5 152.3 all-gather.1
  170.4 128.7 all-reduce.2
  359.7 55.0 all-reduce.4
where the time goes:
time: 476 us
  waiting for transfers between devices  290 us (61%)
  matrix products  158 us (33%)
  between operations  13.8 us (3%)
  other arithmetic  13.3 us (3%)
    all_gather x1, waiting for transfers between devices, per_device(): gathered = lax.all_gather(activations, 'mp', axis=0, tiled=True)  146 us
    psum x1, waiting for transfers between devices, per_device(): p_mean = lax.psum(partial_p, ('dp', 'mp')) / replicas  88.4 us
    psum x1, waiting for transfers between devices, per_device(): q_factor = lax.psum(local_factor, 'dp') / replicas  55.2 us
    dot_general x1, matrix products, per_device(): lax.dot_general(p_ortho, q_factor, (((1,), (1,)), ((), ())), precision=hi...  53.4 us
    dot_general x1, matrix products, per_device(): lax.dot_general(gradient, p_ortho, contract_rows, precision=highest)  43.2 us
    dot_general x1, matrix products, per_device(): lax.dot_general(gathered, output_grads, contract_rows, preferred_element_...  40.3 us
  transfers between devices with their start and end apart: 3, of which 3 were waited for; matrix products, arithmetic and copies ran while one was open for 10% of the time, Pallas kernels for 0%

commit v1 on v0

--- a/solution.py
+++ b/solution.py
@@ -35,7 +35,7 @@
     gradient = lax.dot_general(
         gathered, output_grads, contract_rows, preferred_element_type=jnp.float32
     )
-    p_mean = lax.psum(partial_p, ("dp", "mp")) / replicas
+    p_mean = jnp.sum(lax.all_gather(partial_p, ("dp", "mp")), axis=0) / replicas
     gram_matrix = lax.dot_general(p_mean, p_mean, contract_rows, precision=highest)
     p_ortho = orthonormal(p_mean, gram_matrix)
     local_factor = lax.dot_general(gradient, p_ortho, contract_rows, precision=highest)

time: 476 us -> 570 us (1.20)
  waiting for transfers between devices: 290 us -> 352 us
  local copies, waits for them, and re-layouts: 0.76 us -> 29 us
  other arithmetic: 13.3 us -> 19.5 us
    all_gather x0 -> x1, waiting for transfers between devices: none -> 151 us  [per_device(): p_mean = jnp.sum(lax.all_gather(partial_p, ('dp', 'mp')), axis=0) / replicas]
    psum x1 -> x0, waiting for transfers between devices: 88.4 us -> none  [per_device(): p_mean = lax.psum(partial_p, ('dp', 'mp')) / replicas]
    unnamed x8 -> x9, local copies, waits for them, and re-layouts: 0.68 us -> 28.9 us
    reduce_sum x0 -> x1, other arithmetic: none -> 6.13 us  [per_device(): p_mean = jnp.sum(lax.all_gather(partial_p, ('dp', 'mp')), axis=0) / replicas]
  transfers between devices with their start and end apart: 3 -> 3, of which waited for: 3 -> 3; matrix products, arithmetic and copies ran while one was open for 10% -> 9% of each run, Pallas kernels for 0% -> 0%
where the time goes in v1:
time: 570 us
  waiting for transfers between devices  352 us (62%)
  matrix products  155 us (27%)
  local copies, waits for them, and re-layouts  29 us (5%)
  other arithmetic  19.5 us (3%)
  between operations  13.9 us (2%)
    all_gather x1, waiting for transfers between devices, per_device(): p_mean = jnp.sum(lax.all_gather(partial_p, ('dp', 'mp')), axis=0) / replicas  151 us
    all_gather x1, waiting for transfers between devices, per_device(): gathered = lax.all_gather(activations, 'mp', axis=0, tiled=True)  146 us
    psum x1, waiting for transfers between devices, per_device(): q_factor = lax.psum(local_factor, 'dp') / replicas  54.5 us
    dot_general x1, matrix products, per_device(): lax.dot_general(p_ortho, q_factor, (((1,), (1,)), ((), ())), precision=hi...  53.4 us
    dot_general x1, matrix products, per_device(): lax.dot_general(gradient, p_ortho, contract_rows, precision=highest)  42.9 us
    dot_general x1, matrix products, per_device(): lax.dot_general(gathered, output_grads, contract_rows, preferred_element_...  40.9 us
    unnamed x9, local copies, waits for them, and re-layouts  28.9 us
  transfers between devices with their start and end apart: 3, of which 3 were waited for; matrix products, arithmetic and copies ran while one was open for 9% of the time, Pallas kernels for 0%

profile of v1, /device:TPU:0, one launch (start us, length us, event | category | flops | bytes accessed | tf_op | source)
XLA Modules:
  0.0 570.0 jit_solution(12286166923402952543)
XLA Ops:
  7.2 0.0 copy-start.3
  7.2 0.0 all-gather.4.cloned.1.call-start
  7.2 0.7 all-gather.4.cloned.1.call-update
  7.9 0.0 all-gather.6.cloned.1.call-start
  8.0 0.0 copy-start.1
  8.0 5.7 %fusion.9 = f32[1024,64]{0,1:T(8,128)S(1)} fusion(bf16[1024,3584]{1,0:T(8,128)(2,1)} %param.4, f32[3584,64]{0,1:T(8,128)} %param.5), kind=kOutput, calls=%fused_computation.16 | convolution fusion | flops 469991424 | bytes 8519680 | tf_op jit(solution)/shard_map/dot_general | solution.py:26
  13.7 0.0 copy-done.3
  13.7 0.0 copy-done.1
  13.7 2.3 fusion.1
  16.0 145.9 %all-gather.4.cloned.1.call-done = bf16[1024,4096]{1,0:T(8,128)(2,1)} async-done(((bf16[256,4096]{1,0:T(8,128)(2,1)}), bf16[1024,4096]{1,0:T(8,128)(2,1)}) %all-gather.4.cloned.1.call-update) | async-done | bytes 8388624 | tf_op jit(solution)/shard_map/all_gather | solution.py:24
  161.9 0.0 copy-start
  161.9 5.1 fusion.12
  167.0 0.7 copy-done
  167.7 2.5 fusion
  170.2 0.0 all-gather.6.cloned.1.call-update
  170.3 0.2 all-reduce.2.cloned.1.call-start
  170.5 40.9 %fusion.19 = f32[4096,3584]{1,0:T(8,128)} fusion(bf16[1024,4096]{1,0:T(8,128)(2,1)} %all-gather.4.cloned.1.call-done, bf16[1024,3584]{1,0:T(8,128)(2,1)} %param.4), kind=kOutput, calls=%fused_computation.32 | convolution fusion | flops 30064771072 | bytes 74448896 | tf_op jit(solution)/shard_map/dot_general | solution.py:35
  211.4 151.3 %all-gather.6.cloned.1.call-done = f32[131072,64]{0,1:T(8,128)} async-done(((f32[4096,64]{0,1:T(8,128)}), f32[131072,64]{0,1:T(8,128)}) %all-gather.6.cloned.1.call-update) | async-done | bytes 33554448 | tf_op jit(solution)/shard_map/all_gather | solution.py:38
  362.8 28.2 %copy.7 = f32[8,8,32,4096]{3,2,1,0:T(8,128)S(1)} copy(f32[8,8,32,4096]{3,1,2,0:T(8,128)} %bitcast.30) | data formatting | bytes 67108864
  391.0 6.1 %bitcast_reduce_fusion = f32[4096,64]{0,1:T(8,128)S(1)} fusion(f32[8,8,32,4096]{3,2,1,0:T(8,128)S(1)} %copy.7), kind=kLoop, calls=%fused_computation.1 | loop fusion | flops 8126464 | bytes 34603008 | tf_op jit(solution)/shard_map/reduce_sum | solution.py:38
  397.1 1.0 fusion.4
  398.1 0.1 copy.6
  398.2 5.8 %cholesky.16 = f32[64,64]{1,0:T(8,128)S(1)} custom-call(f32[64,64]{1,0:T(8,128)S(1)} %fusion.16), custom_call_target="Cholesky" | custom-call | tf_op jit(solution)/shard_map/jit(cholesky)/cholesky | solution.py:8
  404.1 0.6 compare_reduce_fusion
  404.7 0.7 fusion.14
  405.4 4.9 custom-call.6
  410.3 1.1 fusion.2
  411.4 42.9 %fusion.20 = f32[3584,64]{0,1:T(8,128)} fusion(f32[4096,3584]{1,0:T(8,128)} %fusion.19, f32[4096,64]{0,1:T(8,128)S(1)} %fusion.2), kind=kOutput, calls=%fused_computation.33 | convolution fusion | flops 11274289152 | bytes 60686336 | tf_op jit(solution)/shard_map/dot_general | solution.py:41
  454.3 0.0 all-reduce.2.cloned.1.call-update
  454.4 54.5 %all-reduce.2.cloned.1.call-done = f32[3584,64]{0,1:T(8,128)} async-done(((f32[3584,64]{0,1:T(8,128)}), f32[3584,64]{0,1:T(8,128)}) %all-reduce.2.cloned.1.call-update) | async-done | bytes 917520 | tf_op jit(solution)/shard_map/psum | solution.py:42
  508.8 1.2 broadcast_multiply_fusion
  510.1 0.0 copy-start.2
  510.1 53.4 %subtract_convert_fusion = bf16[4096,3584]{1,0:T(8,128)(2,1)} fusion(f32[4096,3584]{1,0:T(8,128)} %fusion.19, f32[4096,64]{0,1:T(8,128)S(1)} %fusion.2, f32[3584,64]{0,1:T(8,128)S(1)} %broadcast_multiply_fusion), kind=kOutput, calls=%fused_computation | convolution fusion | flops 11303649280 | bytes 90046464 | tf_op jit(solution)/shard_map/dot_general | solution.py:43
  563.4 0.0 copy-done.2
  (2 shorter events, 0.0 us)
Async XLA Ops:
  7.2 6.5 %copy-start.3 = (f32[3584,64]{0,1:T(8,128)S(1)}, f32[3584,64]{0,1:T(8,128)}, u32[]{:S(2)}) copy-start(f32[3584,64]{0,1:T(8,128)} %param.5) | copy-start | bytes 2752516
  7.2 154.7 %all-gather.4.cloned.1.call-start = ((), (), s32[]{:S(2)}) async-start(), calls=%async_computation | async-start | bytes 10485760 | tf_op jit(solution)/shard_map/all_gather | solution.py:24
  7.9 354.9 %all-gather.6.cloned.1.call-start = ((), (), s32[]{:S(2)}) async-start(), calls=%async_computation.2 | async-start | bytes 34603008 | tf_op jit(solution)/shard_map/all_gather | solution.py:38
  8.0 5.7 %copy-start.1 = (bf16[1024,3584]{1,0:T(8,128)(2,1)S(1)}, bf16[1024,3584]{1,0:T(8,128)(2,1)}, u32[]{:S(2)}) copy-start(bf16[1024,3584]{1,0:T(8,128)(2,1)} %param.4) | copy-start | bytes 22020100
  161.9 5.8 %copy-start = (bf16[1024,4096]{1,0:T(8,128)(2,1)S(1)}, bf16[1024,4096]{1,0:T(8,128)(2,1)}, u32[]{:S(2)}) copy-start(bf16[1024,4096]{1,0:T(8,128)(2,1)} %all-gather.4.cloned.1.call-done) | copy-start | bytes 25165828
  170.3 338.6 %all-reduce.2.cloned.1.call-start = ((), (), s32[]{:S(2)}) async-start(), calls=%async_computation.1 | async-start | bytes 1835008 | tf_op jit(solution)/shard_map/psum | solution.py:42
  510.1 53.4 %copy-start.2 = (f32[3584,64]{0,1:T(8,128)}, f32[3584,64]{0,1:T(8,128)S(1)}, u32[]{:S(2)}) copy-start(f32[3584,64]{0,1:T(8,128)S(1)} %broadcast_multiply_fusion) | copy-start | bytes 2752516
Sparse Core Ops, SparseCore 0:
  9.5 152.3 all-gather.3
  170.4 192.3 all-gather.5
  454.5 54.2 all-reduce.1
